TPU v7x, 256 devices: a whole 4x4x8 slice. The times are simulated.
256 devices in a mesh: band: 8 (over z_hi, y), grid: 32 (over z_lo, x, core).
Axes of the slice: x: 4, y: 4, z: 8 (z_hi: 2, z_lo: 4; z = z_hi * 4 + z_lo), core: 2. Of those that a mesh axis runs over, the one named last changes fastest.
Arguments:
- orbitals: bfloat16 [2048, 65536], P('band', 'grid'), as said below
- projectors: bfloat16 [2048, 65536], P('band', 'grid'), may hold values from -0.015625 to 0.015625
Outputs:
- result: bfloat16 [2048, 65536], P('band', 'grid')
- energies: float32 [2048], P('band')
Inputs may be any that keep to these rules, and one draw needn't show every extreme that they name: The orbitals are real-valued.
All inputs are finite; a program needn't handle non-finite values.
Results may differ from a plain program's by a relative error of at most 0.0049.
Values may be sent and summed in bfloat16 or wider, within the bound.
No kernel may reach another device: no remote copies, remote signals or barrier semaphores. Data moves between devices by JAX's collectives and lax.ppermute only.
A program may use at most 64 MiB of HBM per device.

v0:
```python
import jax
import jax.numpy as jnp
from jax import lax
from jax.sharding import PartitionSpec as P


ZL, NX, NC = 4, 4, 2
ZH, NY = 2, 4


def fetch_band(array, dz, dy):
    pairs = [
        (((z + dz) % ZH) * NY + (y + dy) % NY, z * NY + y)
        for z in range(ZH)
        for y in range(NY)
    ]
    return lax.ppermute(array, "band", pairs)


def grid_pairs(source):
    return [
        (source(zl, x, c), zl * 8 + x * 2 + c)
        for zl in range(ZL)
        for x in range(NX)
        for c in range(NC)
    ]


def from_core(array):
    return lax.ppermute(array, "grid", grid_pairs(lambda zl, x, c: zl * 8 + x * 2 + 1 - c))


def from_x(array, d):
    return lax.ppermute(
        array, "grid", grid_pairs(lambda zl, x, c: zl * 8 + ((x + d) % NX) * 2 + c)
    )


def from_zl(array, d):
    return lax.ppermute(array, "grid", grid_pairs(lambda zl, x, c: (zl ^ d) * 8 + x * 2 + c))


def position():
    g = lax.axis_index("grid")
    return g // 8, (g // 2) % 4, g % 2


def pick(array, at, axis):
    return lax.dynamic_index_in_dim(array, at, axis, keepdims=False)


def reduce_over_x(mine, theirs):
    x = position()[1]
    n, _, cols = mine.shape
    there = from_core(theirs.astype(jnp.bfloat16))
    parts = (mine + there.astype(jnp.float32)).reshape(n, NX, ZL, 8, cols)
    there = []
    for d in (1, 3, 2):
        part = pick(parts, (x + NX - d) % NX, 1).astype(jnp.bfloat16)
        there.append(from_x(part, d))
    return sum((t.astype(jnp.float32) for t in there), pick(parts, x, 1))


def reduce_over_zl(parts):
    zl = position()[0]
    parts = parts.reshape(parts.shape[0], 2, 2, 8, parts.shape[3])
    for d, bit in ((2, zl // 2), (1, zl % 2)):
        there = from_zl(pick(parts, 1 - bit, 1).astype(jnp.bfloat16), d)
        parts = pick(parts, bit, 1) + there.astype(jnp.float32)
    return parts


def placed(pieces, axis):
    length = len(pieces)
    shape = list(pieces[0][1].shape)
    shape.insert(axis, length)
    out = jnp.zeros(shape, pieces[0][1].dtype)
    for at, piece in pieces:
        out = lax.dynamic_update_index_in_dim(out, piece, at, axis)
    return out


def gather_over_grid(rows):
    zl, x, _ = position()
    there = from_zl(rows, 1)
    held = placed([(zl % 2, rows), (1 - zl % 2, there)], 1)
    there = from_zl(held, 2)
    held = placed([(zl // 2, held), (1 - zl // 2, there)], 1)
    held = held.reshape(held.shape[0], ZL, *held.shape[3:])
    there = [((x + d) % NX, from_x(held, d)) for d in (1, 3, 2)]
    held = placed([(x, held)] + there, 1)
    return held, from_core(held)


def intersect(rows, state):
    return lax.dot_general(
        rows, state, (((1,), (1,)), ((), ())), preferred_element_type=jnp.float32
    )


def apply(rounded, rows):
    return lax.dot_general(
        rounded, rows, (((0,), (0,)), ((), ())), preferred_element_type=jnp.float32
    )


def halves(value):
    high = lax.reduce_precision(value, 8, 7)
    return high.astype(jnp.bfloat16), (value - high).astype(jnp.bfloat16)


def gather_projectors(mine):
    up = fetch_band(mine, 0, 1)
    down = fetch_band(mine, 0, 3)
    over = fetch_band(mine, 1, 0)
    up_up = fetch_band(up, 0, 1)
    over_up = fetch_band(over, 0, 1)
    over_down = fetch_band(over, 0, 3)
    last = [fetch_band(over_up[:128], 0, 1), fetch_band(over_down[128:], 0, 3)]
    last = jnp.concatenate(last)
    return [[mine], [up], [up_up], [down]], [[over], [over_up], [last], [over_down]]


def gather_gram(rows):
    c = position()[2]
    pair = jnp.stack([rows, fetch_band(rows, 1, 0)])
    pairs = [pair] + [fetch_band(pair, 0, d) for d in (1, 2, 3)]
    near, far = [], []
    for z in range(ZH):
        for y in range(NY):
            block = jnp.roll(pairs[y][z], (z, y), axis=(0, 1))
            near.append(jnp.where(c == 0, block[..., :128], block[..., 128:]))
            far.append(jnp.where(c == 0, block[..., 128:], block[..., :128]))
    return [jnp.concatenate(h, axis=-1).reshape(64, 1024) for h in (near, far)]


ARRIVAL = (0, 1, 3, 2)


def by_core(blocks):
    c = position()[2]
    blocks = blocks.reshape(-1, 2, 128, blocks.shape[-1])
    return pick(blocks, c, 1), pick(blocks, 1 - c, 1)


def per_device(orbitals, projectors):
    total_bands = projectors.shape[0] * lax.axis_size("band")
    total_points = projectors.shape[1] * lax.axis_size("grid")
    square = jnp.sum(jnp.square(orbitals.astype(jnp.float32)), axis=1)
    plane, beyond = gather_projectors(projectors)

    states = jnp.concatenate([orbitals, projectors])
    terms = [intersect(plane[y][0], states) for y in ARRIVAL]
    here = reduce_over_x(*by_core(jnp.concatenate(terms)))
    terms = [intersect(rows, states) for y in ARRIVAL for rows in beyond[y]]
    there = reduce_over_x(*by_core(jnp.concatenate(terms)))
    sums = reduce_over_zl(jnp.concatenate([here, there]))
    sums = sums.reshape(ZH, NY, 8, 512)
    sums = jnp.stack([sums[:, ARRIVAL.index(y)] for y in range(NY)], axis=1).reshape(8, 8, 512)
    first, gram = sums[..., :256], sums[..., 256:]
    gram_near, gram_far = gather_gram(gram.astype(jnp.bfloat16).reshape(ZH, NY, 8, 256))

    blocks = [rows for part in (plane, beyond) for y in range(NY) for rows in part[y]]
    near, far = by_core(jnp.concatenate(blocks))
    near, far = near.reshape(1024, -1), far.reshape(1024, -1)

    first_b = first.astype(jnp.bfloat16)
    mine, other = gather_over_grid(first_b)
    mine, other = mine.reshape(1024, 256), other.reshape(1024, 256)
    first, first_b = first.reshape(64, 256), first_b.reshape(64, 256)
    second = first - jnp.dot(gram_near, mine, preferred_element_type=jnp.float32)
    second = second - jnp.dot(gram_far, other, preferred_element_type=jnp.float32)
    second_b = second.astype(jnp.bfloat16)
    value = jnp.sum(second * second_b.astype(jnp.float32), axis=0)
    norm = square - jnp.sum(first_b.astype(jnp.float32) * (first + second), axis=0)

    middle = orbitals.astype(jnp.float32) - apply(mine, near)
    widened = lax.reduce_precision(middle - apply(other, far), 8, 7)

    sums = jnp.stack([*halves(value), *halves(norm)])
    sums = jnp.concatenate([sums, jnp.zeros((4, 256), jnp.bfloat16)])
    rows = jnp.concatenate([second_b.reshape(8, 8, 256), sums[None]])
    mine, other = gather_over_grid(rows)
    sums = sum(h[8, ..., :4, :].astype(jnp.float32).sum(axis=(0, 1)) for h in (mine, other))
    result = widened - apply(mine[:8].reshape(1024, 256), near)
    result = (result - apply(other[:8].reshape(1024, 256), far)).astype(jnp.bfloat16)
    energies = 2.0 * total_points / total_bands * (sums[0] + sums[1]) / (sums[2] + sums[3])
    return (result, energies)


def solution(mesh):
    in_specs = (P("band", "grid"), P("band", "grid"))
    out_specs = (P("band", "grid"), P("band"))
    return jax.shard_map(
        per_device, mesh=mesh, in_specs=in_specs, out_specs=out_specs, check_vma=False
    )
```

profile of v0, /device:TPU:1, one launch (start us, length us, event | category | flops | bytes accessed | tf_op | source)
XLA Modules:
  0.0 209.3 jit_solution(13880309507991243781)
XLA Ops:
  0.6 7.8 %collective-permute-start.7 = (bf16[256,2048]{1,0:T(8,128)(2,1)}, bf16[256,2048]{1,0:T(8,128)(2,1)S(1)}, u32[]{:S(2)}, u32[]{:S(2)}) collective-permute-start(bf16[256,2048]{1,0:T(8,128)(2,1)} %param.3), channel_id=1, source_target_pairs={{128,0},{160,32},{192,64},{224,96},{0,128},{32,160},{64,192},{96,2... | collective-permute-start | bytes 3145736 | tf_op jit(solution)/shard_map/ppermute | solution.py:17
  8.5 2.7 %collective-permute-start = (bf16[256,2048]{1,0:T(8,128)(2,1)}, bf16[256,2048]{1,0:T(8,128)(2,1)}, u32[]{:S(2)}, u32[]{:S(2)}) collective-permute-start(bf16[256,2048]{1,0:T(8,128)(2,1)} %param.3), channel_id=1, source_target_pairs={{32,0},{64,32},{96,64},{0,96},{160,128},{192,160},{224,192},{128,2... | collective-permute-start | bytes 3145736 | tf_op jit(solution)/shard_map/ppermute | solution.py:17
  14.2 22.8 %collective-permute-done.7 = bf16[256,2048]{1,0:T(8,128)(2,1)S(1)} collective-permute-done((bf16[256,2048]{1,0:T(8,128)(2,1)}, bf16[256,2048]{1,0:T(8,128)(2,1)S(1)}, u32[]{:S(2)}, u32[]{:S(2)}) %collective-permute-start.7) | collective-permute-done | bytes 1048608 | tf_op jit(solution)/shard_map/ppermute | solution.py:17
  47.8 4.7 %collective-permute-done.9 = bf16[256,2048]{1,0:T(8,128)(2,1)S(1)} collective-permute-done((bf16[256,2048]{1,0:T(8,128)(2,1)S(1)}, bf16[256,2048]{1,0:T(8,128)(2,1)S(1)}, u32[]{:S(2)}, u32[]{:S(2)}) %collective-permute-start.9) | collective-permute-done | bytes 1048608 | tf_op jit(solution)/shard_map/ppermute | solution.py:17
  52.6 2.7 %collective-permute-start.10 = (bf16[128,2048]{1,0:T(8,128)(2,1)S(1)}, bf16[128,2048]{1,0:T(8,128)(2,1)S(1)}, u32[]{:S(2)}, u32[]{:S(2)}) collective-permute-start(bf16[128,2048]{1,0:T(8,128)(2,1)S(1)} %slice.288), channel_id=1, source_target_pairs={{32,0},{64,32},{96,64},{0,96},{160,128},{192,160},{224,192},{128,2... | collective-permute-start | bytes 1572872 | tf_op jit(solution)/shard_map/ppermute | solution.py:17
  55.3 13.8 %collective-permute-done.2 = bf16[256,2048]{1,0:T(8,128)(2,1)S(1)} collective-permute-done((bf16[256,2048]{1,0:T(8,128)(2,1)}, bf16[256,2048]{1,0:T(8,128)(2,1)S(1)}, u32[]{:S(2)}, u32[]{:S(2)}) %collective-permute-start.2) | collective-permute-done | bytes 1048608 | tf_op jit(solution)/shard_map/ppermute | solution.py:17
  70.2 23.6 %collective-permute-start.3 = (bf16[4,128,512]{2,1,0:T(8,128)(2,1)S(1)}, bf16[4,128,512]{2,1,0:T(8,128)(2,1)S(1)}, u32[]{:S(2)}, u32[]{:S(2)}) collective-permute-start(bf16[4,128,512]{2,1,0:T(8,128)(2,1)S(1)} %fusion.9), channel_id=1, source_target_pairs={{1,0},{0,1},{3,2},{2,3},{5,4},{4,5},{7,6},{6,7},{9,8},{8,9},{11,10... | collective-permute-start | bytes 1572872 | tf_op jit(solution)/shard_map/ppermute | solution.py:30
  99.4 2.8 %collective-permute-start.6 = (bf16[4,4,8,512]{3,2,1,0:T(8,128)(2,1)S(1)}, bf16[4,4,8,512]{3,2,1,0:T(8,128)(2,1)S(1)}, u32[]{:S(2)}, u32[]{:S(2)}) collective-permute-start(bf16[4,4,8,512]{3,2,1,0:T(8,128)(2,1)S(1)} %get-tuple-element.11), channel_id=1, source_target_pairs={{4,0},{5,1},{6,2},{7,3},{0,4},{1,5},{2,6},{3,7},{12,8},{13,9},{14,... | collective-permute-start | bytes 393224 | tf_op jit(solution)/shard_map/ppermute | solution.py:34
  111.2 3.5 %collective-permute-done.14 = bf16[4,4,8,512]{3,2,1,0:T(8,128)(2,1)S(1)} collective-permute-done((bf16[4,4,8,512]{3,2,1,0:T(8,128)(2,1)S(1)}, bf16[4,4,8,512]{3,2,1,0:T(8,128)(2,1)S(1)}, u32[]{:S(2)}, u32[]{:S(2)}) %collective-permute-start.14) | collective-permute-done | bytes 131104 | tf_op jit(solution)/shard_map/ppermute | solution.py:34
  114.9 18.2 %collective-permute-start.16 = (bf16[8,2,8,512]{3,2,1,0:T(8,128)(2,1)S(1)}, bf16[8,2,8,512]{3,2,1,0:T(8,128)(2,1)S(1)}, u32[]{:S(2)}, u32[]{:S(2)}) collective-permute-start(bf16[8,2,8,512]{3,2,1,0:T(8,128)(2,1)S(1)} %fusion.16), channel_id=1, source_target_pairs={{16,0},{17,1},{18,2},{19,3},{20,4},{21,5},{22,6},{23,7},{24,8},{25... | collective-permute-start | bytes 393224 | tf_op jit(solution)/shard_map/ppermute | solution.py:40
  133.1 5.9 %collective-permute-done.16 = bf16[8,2,8,512]{3,2,1,0:T(8,128)(2,1)S(1)} collective-permute-done((bf16[8,2,8,512]{3,2,1,0:T(8,128)(2,1)S(1)}, bf16[8,2,8,512]{3,2,1,0:T(8,128)(2,1)S(1)}, u32[]{:S(2)}, u32[]{:S(2)}) %collective-permute-start.16) | collective-permute-done | bytes 131104 | tf_op jit(solution)/shard_map/ppermute | solution.py:40
  139.2 4.1 %constant_dynamic-slice_fusion.1 = (bf16[8,1,128,2048]{3,2,1,0:T(8,128)(2,1)}, bf16[8,1,128,2048]{3,2,1,0:T(8,128)(2,1)}) fusion(bf16[8,2,128,2048]{3,2,1,0:T(8,128)(2,1)S(1)} %bitcast.212, s32[]{:T(128)S(6)} %select_n.218, s32[]{:T(128)S(6)} %select_n.219), kind=kLoop, calls=%fused_computation.148 | loop fusion | bytes 16777224 | tf_op jit(solution)/shard_map/jit(dynamic_index_in_dim)/dynamic_slice | solution.py:49
  145.0 4.6 %collective-permute-start.24 = (bf16[2,4,8,256]{3,2,1,0:T(8,128)(2,1)S(1)}, bf16[2,4,8,256]{3,2,1,0:T(8,128)(2,1)S(1)}, u32[]{:S(2)}, u32[]{:S(2)}) collective-permute-start(bf16[2,4,8,256]{3,2,1,0:T(8,128)(2,1)S(1)} %bitcast.244), channel_id=1, source_target_pairs={{128,0},{160,32},{192,64},{224,96},{0,128},{32,160},{64,192},{96,2... | collective-permute-start | bytes 98312 | tf_op jit(solution)/shard_map/ppermute | solution.py:17
  151.6 2.7 %collective-permute-start.25 = (bf16[2,2,4,8,256]{4,3,2,1,0:T(8,128)(2,1)S(1)}, bf16[2,2,4,8,256]{4,3,2,1,0:T(8,128)(2,1)S(1)}, u32[]{:S(2)}, u32[]{:S(2)}) collective-permute-start(bf16[2,2,4,8,256]{4,3,2,1,0:T(8,128)(2,1)S(1)} %pad_maximum_fusion.4), channel_id=1, source_target_pairs={{32,0},{64,32},{96,64},{0,96},{160,128},{192,160},{224,192},{128,2... | collective-permute-start | bytes 196616 | tf_op jit(solution)/shard_map/ppermute | solution.py:17
  155.5 4.4 %collective-permute-done.19 = bf16[8,2,8,256]{3,2,1,0:T(8,128)(2,1)S(1)} collective-permute-done((bf16[8,2,8,256]{3,2,1,0:T(8,128)(2,1)S(1)}, bf16[8,2,8,256]{3,2,1,0:T(8,128)(2,1)S(1)}, u32[]{:S(2)}, u32[]{:S(2)}) %collective-permute-start.19) | collective-permute-done | bytes 65568 | tf_op jit(solution)/shard_map/ppermute | solution.py:40
  159.9 3.2 %collective-permute-start.20 = (bf16[8,4,8,256]{3,2,1,0:T(8,128)(2,1)S(1)}, bf16[8,4,8,256]{3,2,1,0:T(8,128)(2,1)S(1)}, u32[]{:S(2)}, u32[]{:S(2)}) collective-permute-start(bf16[8,4,8,256]{3,2,1,0:T(8,128)(2,1)S(1)} %bitcast.237), channel_id=1, source_target_pairs={{2,0},{3,1},{4,2},{5,3},{6,4},{7,5},{0,6},{1,7},{10,8},{11,9},{12,... | collective-permute-start | bytes 393224 | tf_op jit(solution)/shard_map/ppermute | solution.py:34
  165.0 4.5 %collective-permute-done.21 = bf16[8,4,8,256]{3,2,1,0:T(8,128)(2,1)S(1)} collective-permute-done((bf16[8,4,8,256]{3,2,1,0:T(8,128)(2,1)S(1)}, bf16[8,4,8,256]{3,2,1,0:T(8,128)(2,1)S(1)}, u32[]{:S(2)}, u32[]{:S(2)}) %collective-permute-start.21) | collective-permute-done | bytes 131104 | tf_op jit(solution)/shard_map/ppermute | solution.py:34
  169.5 5.9 %collective-permute-start.23 = (bf16[8,4,4,8,256]{4,3,2,1,0:T(8,128)(2,1)S(1)}, bf16[8,4,4,8,256]{4,3,2,1,0:T(8,128)(2,1)S(1)}, u32[]{:S(2)}, u32[]{:S(2)}) collective-permute-start(bf16[8,4,4,8,256]{4,3,2,1,0:T(8,128)(2,1)S(1)} %bitcast_dynamic-update-slice_fusion.6), channel_id=1, source_target_pairs={{1,0},{0,1},{3,2},{2,3},{5,4},{4,5},{7,6},{6,7},{9,8},{8,9},{11,10... | collective-permute-start | bytes 1572872 | tf_op jit(solution)/shard_map/ppermute | solution.py:30
  177.0 2.6 %fusion.41 = f32[256,2048]{1,0:T(8,128)} fusion(bf16[1024,256]{1,0:T(8,128)(2,1)S(1)} %bitcast.234, bf16[1024,2048]{1,0:T(8,128)(2,1)S(1)} %bitcast.219), kind=kOutput, calls=%fused_computation.163 | convolution fusion | flops 1073741824 | bytes 6815744 | tf_op jit(solution)/shard_map/dot_general | solution.py:102
  180.3 2.8 %collective-permute-done.28 = bf16[9,8,256]{2,1,0:T(8,128)(2,1)S(1)} collective-permute-done((bf16[9,8,256]{2,1,0:T(8,128)(2,1)S(1)}, bf16[9,8,256]{2,1,0:T(8,128)(2,1)S(1)}, u32[]{:S(2)}, u32[]{:S(2)}) %collective-permute-start.28) | collective-permute-done | bytes 36896 | tf_op jit(solution)/shard_map/ppermute | solution.py:40
  183.6 4.1 %collective-permute-done.29 = bf16[9,2,8,256]{3,2,1,0:T(8,128)(2,1)S(1)} collective-permute-done((bf16[9,2,8,256]{3,2,1,0:T(8,128)(2,1)S(1)}, bf16[9,2,8,256]{3,2,1,0:T(8,128)(2,1)S(1)}, u32[]{:S(2)}, u32[]{:S(2)}) %collective-permute-start.29) | collective-permute-done | bytes 73760 | tf_op jit(solution)/shard_map/ppermute | solution.py:40
  189.6 4.3 %fusion.1 = f32[256,2048]{1,0:T(8,128)S(1)} fusion(f32[256,2048]{1,0:T(8,128)} %fusion.41, bf16[1024,256]{1,0:T(8,128)(2,1)S(1)} %bitcast.214, bf16[1024,2048]{1,0:T(8,128)(2,1)} %bitcast.210, bf16[256,2048]{1,0:T(8,128)(2,1)S(1)} %copy-done.1), kind=kOutput, calls=%fused_computation.5 | convolution fusion | flops 1075838976 | bytes 9961472 | tf_op jit(solution)/shard_map/dot_general | solution.py:102
  195.3 5.8 %collective-permute-done.31 = bf16[9,4,8,256]{3,2,1,0:T(8,128)(2,1)S(1)} collective-permute-done((bf16[9,4,8,256]{3,2,1,0:T(8,128)(2,1)S(1)}, bf16[9,4,8,256]{3,2,1,0:T(8,128)(2,1)S(1)}, u32[]{:S(2)}, u32[]{:S(2)}) %collective-permute-start.31) | collective-permute-done | bytes 147488 | tf_op jit(solution)/shard_map/ppermute | solution.py:34
  201.2 3.6 %collective-permute-start.33 = (bf16[9,4,4,8,256]{4,3,2,1,0:T(8,128)(2,1)S(1)}, bf16[9,4,4,8,256]{4,3,2,1,0:T(8,128)(2,1)S(1)}, u32[]{:S(2)}, u32[]{:S(2)}) collective-permute-start(bf16[9,4,4,8,256]{4,3,2,1,0:T(8,128)(2,1)S(1)} %bitcast_dynamic-update-slice_fusion.2), channel_id=1, source_target_pairs={{1,0},{0,1},{3,2},{2,3},{5,4},{4,5},{7,6},{6,7},{9,8},{8,9},{11,10... | collective-permute-start | bytes 1769480 | tf_op jit(solution)/shard_map/ppermute | solution.py:30
  (160 shorter events, 46.8 us)
Async XLA Ops:
  0.6 36.4 %collective-permute-start.7 = (bf16[256,2048]{1,0:T(8,128)(2,1)}, bf16[256,2048]{1,0:T(8,128)(2,1)S(1)}, u32[]{:S(2)}, u32[]{:S(2)}) collective-permute-start(bf16[256,2048]{1,0:T(8,128)(2,1)} %param.3), channel_id=1, source_target_pairs={{128,0},{160,32},{192,64},{224,96},{0,128},{32,160},{64,192},{96,2... | collective-permute-start | bytes 3145736 | tf_op jit(solution)/shard_map/ppermute | solution.py:17
  8.5 31.8 %collective-permute-start = (bf16[256,2048]{1,0:T(8,128)(2,1)}, bf16[256,2048]{1,0:T(8,128)(2,1)}, u32[]{:S(2)}, u32[]{:S(2)}) collective-permute-start(bf16[256,2048]{1,0:T(8,128)(2,1)} %param.3), channel_id=1, source_target_pairs={{32,0},{64,32},{96,64},{0,96},{160,128},{192,160},{224,192},{128,2... | collective-permute-start | bytes 3145736 | tf_op jit(solution)/shard_map/ppermute | solution.py:17
  11.2 34.6 %collective-permute-start.1 = (bf16[256,2048]{1,0:T(8,128)(2,1)}, bf16[256,2048]{1,0:T(8,128)(2,1)}, u32[]{:S(2)}, u32[]{:S(2)}) collective-permute-start(bf16[256,2048]{1,0:T(8,128)(2,1)} %param.3), channel_id=1, source_target_pairs={{96,0},{0,32},{32,64},{64,96},{224,128},{128,160},{160,192},{192,2... | collective-permute-start | bytes 3145736 | tf_op jit(solution)/shard_map/ppermute | solution.py:17
  37.1 15.4 %collective-permute-start.9 = (bf16[256,2048]{1,0:T(8,128)(2,1)S(1)}, bf16[256,2048]{1,0:T(8,128)(2,1)S(1)}, u32[]{:S(2)}, u32[]{:S(2)}) collective-permute-start(bf16[256,2048]{1,0:T(8,128)(2,1)S(1)} %collective-permute-done.7), channel_id=1, source_target_pairs={{96,0},{0,32},{32,64},{64,96},{224,128},{128,160},{160,192},{192,2... | collective-permute-start | bytes 3145736 | tf_op jit(solution)/shard_map/ppermute | solution.py:17
  38.8 13.8 %collective-permute-start.8 = (bf16[256,2048]{1,0:T(8,128)(2,1)S(1)}, bf16[256,2048]{1,0:T(8,128)(2,1)S(1)}, u32[]{:S(2)}, u32[]{:S(2)}) collective-permute-start(bf16[256,2048]{1,0:T(8,128)(2,1)S(1)} %collective-permute-done.7), channel_id=1, source_target_pairs={{32,0},{64,32},{96,64},{0,96},{160,128},{192,160},{224,192},{128,2... | collective-permute-start | bytes 3145736 | tf_op jit(solution)/shard_map/ppermute | solution.py:17
  40.3 28.9 %collective-permute-start.2 = (bf16[256,2048]{1,0:T(8,128)(2,1)}, bf16[256,2048]{1,0:T(8,128)(2,1)S(1)}, u32[]{:S(2)}, u32[]{:S(2)}) collective-permute-start(bf16[256,2048]{1,0:T(8,128)(2,1)} %collective-permute-done), channel_id=1, source_target_pairs={{32,0},{64,32},{96,64},{0,96},{160,128},{192,160},{224,192},{128,2... | collective-permute-start | bytes 3145736 | tf_op jit(solution)/shard_map/ppermute | solution.py:17
  52.5 44.4 %collective-permute-start.11 = (bf16[128,2048]{1,0:T(8,128)(2,1)S(1)}, bf16[128,2048]{1,0:T(8,128)(2,1)S(1)}, u32[]{:S(2)}, u32[]{:S(2)}) collective-permute-start(bf16[128,2048]{1,0:T(8,128)(2,1)S(1)} %slice.289), channel_id=1, source_target_pairs={{96,0},{0,32},{32,64},{64,96},{224,128},{128,160},{160,192},{192,2... | collective-permute-start | bytes 1572872 | tf_op jit(solution)/shard_map/ppermute | solution.py:17
  52.6 44.3 %collective-permute-start.10 = (bf16[128,2048]{1,0:T(8,128)(2,1)S(1)}, bf16[128,2048]{1,0:T(8,128)(2,1)S(1)}, u32[]{:S(2)}, u32[]{:S(2)}) collective-permute-start(bf16[128,2048]{1,0:T(8,128)(2,1)S(1)} %slice.288), channel_id=1, source_target_pairs={{32,0},{64,32},{96,64},{0,96},{160,128},{192,160},{224,192},{128,2... | collective-permute-start | bytes 1572872 | tf_op jit(solution)/shard_map/ppermute | solution.py:17
  70.2 29.0 %collective-permute-start.3 = (bf16[4,128,512]{2,1,0:T(8,128)(2,1)S(1)}, bf16[4,128,512]{2,1,0:T(8,128)(2,1)S(1)}, u32[]{:S(2)}, u32[]{:S(2)}) collective-permute-start(bf16[4,128,512]{2,1,0:T(8,128)(2,1)S(1)} %fusion.9), channel_id=1, source_target_pairs={{1,0},{0,1},{3,2},{2,3},{5,4},{4,5},{7,6},{6,7},{9,8},{8,9},{11,10... | collective-permute-start | bytes 1572872 | tf_op jit(solution)/shard_map/ppermute | solution.py:30
  97.9 7.1 %collective-permute-start.12 = (bf16[4,128,512]{2,1,0:T(8,128)(2,1)S(1)}, bf16[4,128,512]{2,1,0:T(8,128)(2,1)S(1)}, u32[]{:S(2)}, u32[]{:S(2)}) collective-permute-start(bf16[4,128,512]{2,1,0:T(8,128)(2,1)S(1)} %fusion.10), channel_id=1, source_target_pairs={{1,0},{0,1},{3,2},{2,3},{5,4},{4,5},{7,6},{6,7},{9,8},{8,9},{11,10... | collective-permute-start | bytes 1572872 | tf_op jit(solution)/shard_map/ppermute | solution.py:30
  99.4 6.6 %collective-permute-start.6 = (bf16[4,4,8,512]{3,2,1,0:T(8,128)(2,1)S(1)}, bf16[4,4,8,512]{3,2,1,0:T(8,128)(2,1)S(1)}, u32[]{:S(2)}, u32[]{:S(2)}) collective-permute-start(bf16[4,4,8,512]{3,2,1,0:T(8,128)(2,1)S(1)} %get-tuple-element.11), channel_id=1, source_target_pairs={{4,0},{5,1},{6,2},{7,3},{0,4},{1,5},{2,6},{3,7},{12,8},{13,9},{14,... | collective-permute-start | bytes 393224 | tf_op jit(solution)/shard_map/ppermute | solution.py:34
  102.3 6.8 %collective-permute-start.5 = (bf16[4,4,8,512]{3,2,1,0:T(8,128)(2,1)S(1)}, bf16[4,4,8,512]{3,2,1,0:T(8,128)(2,1)S(1)}, u32[]{:S(2)}, u32[]{:S(2)}) collective-permute-start(bf16[4,4,8,512]{3,2,1,0:T(8,128)(2,1)S(1)} %get-tuple-element.12), channel_id=1, source_target_pairs={{6,0},{7,1},{0,2},{1,3},{2,4},{3,5},{4,6},{5,7},{14,8},{15,9},{8,1... | collective-permute-start | bytes 393224 | tf_op jit(solution)/shard_map/ppermute | solution.py:34
  105.4 9.3 %collective-permute-start.14 = (bf16[4,4,8,512]{3,2,1,0:T(8,128)(2,1)S(1)}, bf16[4,4,8,512]{3,2,1,0:T(8,128)(2,1)S(1)}, u32[]{:S(2)}, u32[]{:S(2)}) collective-permute-start(bf16[4,4,8,512]{3,2,1,0:T(8,128)(2,1)S(1)} %get-tuple-element.14), channel_id=1, source_target_pairs={{6,0},{7,1},{0,2},{1,3},{2,4},{3,5},{4,6},{5,7},{14,8},{15,9},{8,1... | collective-permute-start | bytes 393224 | tf_op jit(solution)/shard_map/ppermute | solution.py:34
  106.1 8.7 %collective-permute-start.13 = (bf16[4,4,8,512]{3,2,1,0:T(8,128)(2,1)S(1)}, bf16[4,4,8,512]{3,2,1,0:T(8,128)(2,1)S(1)}, u32[]{:S(2)}, u32[]{:S(2)}) collective-permute-start(bf16[4,4,8,512]{3,2,1,0:T(8,128)(2,1)S(1)} %get-tuple-element.13), channel_id=1, source_target_pairs={{2,0},{3,1},{4,2},{5,3},{6,4},{7,5},{0,6},{1,7},{10,8},{11,9},{12,... | collective-permute-start | bytes 393224 | tf_op jit(solution)/shard_map/ppermute | solution.py:34
  114.9 24.1 %collective-permute-start.16 = (bf16[8,2,8,512]{3,2,1,0:T(8,128)(2,1)S(1)}, bf16[8,2,8,512]{3,2,1,0:T(8,128)(2,1)S(1)}, u32[]{:S(2)}, u32[]{:S(2)}) collective-permute-start(bf16[8,2,8,512]{3,2,1,0:T(8,128)(2,1)S(1)} %fusion.16), channel_id=1, source_target_pairs={{16,0},{17,1},{18,2},{19,3},{20,4},{21,5},{22,6},{23,7},{24,8},{25... | collective-permute-start | bytes 393224 | tf_op jit(solution)/shard_map/ppermute | solution.py:40
  143.4 11.8 %collective-permute-start.18 = (bf16[8,8,256]{2,1,0:T(8,128)(2,1)S(1)}, bf16[8,8,256]{2,1,0:T(8,128)(2,1)S(1)}, u32[]{:S(2)}, u32[]{:S(2)}) collective-permute-start(bf16[8,8,256]{2,1,0:T(8,128)(2,1)S(1)} %get-tuple-element.5), channel_id=1, source_target_pairs={{8,0},{9,1},{10,2},{11,3},{12,4},{13,5},{14,6},{15,7},{0,8},{1,9},... | collective-permute-start | bytes 98312 | tf_op jit(solution)/shard_map/ppermute | solution.py:40
  145.0 6.7 %collective-permute-start.24 = (bf16[2,4,8,256]{3,2,1,0:T(8,128)(2,1)S(1)}, bf16[2,4,8,256]{3,2,1,0:T(8,128)(2,1)S(1)}, u32[]{:S(2)}, u32[]{:S(2)}) collective-permute-start(bf16[2,4,8,256]{3,2,1,0:T(8,128)(2,1)S(1)} %bitcast.244), channel_id=1, source_target_pairs={{128,0},{160,32},{192,64},{224,96},{0,128},{32,160},{64,192},{96,2... | collective-permute-start | bytes 98312 | tf_op jit(solution)/shard_map/ppermute | solution.py:17
  151.6 11.4 %collective-permute-start.25 = (bf16[2,2,4,8,256]{4,3,2,1,0:T(8,128)(2,1)S(1)}, bf16[2,2,4,8,256]{4,3,2,1,0:T(8,128)(2,1)S(1)}, u32[]{:S(2)}, u32[]{:S(2)}) collective-permute-start(bf16[2,2,4,8,256]{4,3,2,1,0:T(8,128)(2,1)S(1)} %pad_maximum_fusion.4), channel_id=1, source_target_pairs={{32,0},{64,32},{96,64},{0,96},{160,128},{192,160},{224,192},{128,2... | collective-permute-start | bytes 196616 | tf_op jit(solution)/shard_map/ppermute | solution.py:17
  154.4 10.0 %collective-permute-start.26 = (bf16[2,2,4,8,256]{4,3,2,1,0:T(8,128)(2,1)S(1)}, bf16[2,2,4,8,256]{4,3,2,1,0:T(8,128)(2,1)S(1)}, u32[]{:S(2)}, u32[]{:S(2)}) collective-permute-start(bf16[2,2,4,8,256]{4,3,2,1,0:T(8,128)(2,1)S(1)} %pad_maximum_fusion.4), channel_id=1, source_target_pairs={{64,0},{96,32},{0,64},{32,96},{192,128},{224,160},{128,192},{160,2... | collective-permute-start | bytes 196616 | tf_op jit(solution)/shard_map/ppermute | solution.py:17
  154.8 9.5 %collective-permute-start.27 = (bf16[2,2,4,8,256]{4,3,2,1,0:T(8,128)(2,1)S(1)}, bf16[2,2,4,8,256]{4,3,2,1,0:T(8,128)(2,1)S(1)}, u32[]{:S(2)}, u32[]{:S(2)}) collective-permute-start(bf16[2,2,4,8,256]{4,3,2,1,0:T(8,128)(2,1)S(1)} %pad_maximum_fusion.4), channel_id=1, source_target_pairs={{96,0},{0,32},{32,64},{64,96},{224,128},{128,160},{160,192},{192,2... | collective-permute-start | bytes 196616 | tf_op jit(solution)/shard_map/ppermute | solution.py:17
  169.5 7.5 %collective-permute-start.23 = (bf16[8,4,4,8,256]{4,3,2,1,0:T(8,128)(2,1)S(1)}, bf16[8,4,4,8,256]{4,3,2,1,0:T(8,128)(2,1)S(1)}, u32[]{:S(2)}, u32[]{:S(2)}) collective-permute-start(bf16[8,4,4,8,256]{4,3,2,1,0:T(8,128)(2,1)S(1)} %bitcast_dynamic-update-slice_fusion.6), channel_id=1, source_target_pairs={{1,0},{0,1},{3,2},{2,3},{5,4},{4,5},{7,6},{6,7},{9,8},{8,9},{11,10... | collective-permute-start | bytes 1572872 | tf_op jit(solution)/shard_map/ppermute | solution.py:30
  187.7 7.6 %collective-permute-start.30 = (bf16[9,4,8,256]{3,2,1,0:T(8,128)(2,1)S(1)}, bf16[9,4,8,256]{3,2,1,0:T(8,128)(2,1)S(1)}, u32[]{:S(2)}, u32[]{:S(2)}) collective-permute-start(bf16[9,4,8,256]{3,2,1,0:T(8,128)(2,1)S(1)} %bitcast.228), channel_id=1, source_target_pairs={{2,0},{3,1},{4,2},{5,3},{6,4},{7,5},{0,6},{1,7},{10,8},{11,9},{12,... | collective-permute-start | bytes 442376 | tf_op jit(solution)/shard_map/ppermute | solution.py:34
  193.9 7.2 %collective-permute-start.31 = (bf16[9,4,8,256]{3,2,1,0:T(8,128)(2,1)S(1)}, bf16[9,4,8,256]{3,2,1,0:T(8,128)(2,1)S(1)}, u32[]{:S(2)}, u32[]{:S(2)}) collective-permute-start(bf16[9,4,8,256]{3,2,1,0:T(8,128)(2,1)S(1)} %bitcast.229), channel_id=1, source_target_pairs={{6,0},{7,1},{0,2},{1,3},{2,4},{3,5},{4,6},{5,7},{14,8},{15,9},{8,1... | collective-permute-start | bytes 442376 | tf_op jit(solution)/shard_map/ppermute | solution.py:34
  194.0 7.1 %collective-permute-start.32 = (bf16[9,4,8,256]{3,2,1,0:T(8,128)(2,1)S(1)}, bf16[9,4,8,256]{3,2,1,0:T(8,128)(2,1)S(1)}, u32[]{:S(2)}, u32[]{:S(2)}) collective-permute-start(bf16[9,4,8,256]{3,2,1,0:T(8,128)(2,1)S(1)} %bitcast.230), channel_id=1, source_target_pairs={{4,0},{5,1},{6,2},{7,3},{0,4},{1,5},{2,6},{3,7},{12,8},{13,9},{14,... | collective-permute-start | bytes 442376 | tf_op jit(solution)/shard_map/ppermute | solution.py:34
  (15 other events, 116.2 us)
where the time goes:
time: 210 us; the launch traced here: 209 us
  starting transfers between devices  97.5 us (46%)
  waiting for transfers between devices  79 us (38%)
  matrix products  19.3 us (9%)
  local copies, waits for them, and re-layouts  10.1 us (5%)
  other arithmetic  2.12 us (1%)
    ppermute x12, waiting for transfers between devices, fetch_band(): return lax.ppermute(array, 'band', pairs)  43.4 us
    ppermute x4, starting transfers between devices, from_core(): lax.ppermute(array, 'grid', grid_pairs(lambda zl, x, c: zl * 8 + x * 2 +...  34.5 us
    ppermute x12, starting transfers between devices, fetch_band(): return lax.ppermute(array, 'band', pairs)  26.2 us
    ppermute x6, starting transfers between devices, from_zl(): lax.ppermute(array, 'grid', grid_pairs(lambda zl, x, c: (zl ^ d) * 8 + x...  20.6 us
    ppermute x6, waiting for transfers between devices, from_zl(): lax.ppermute(array, 'grid', grid_pairs(lambda zl, x, c: (zl ^ d) * 8 + x...  17.1 us
    ppermute x12, waiting for transfers between devices, from_x(): lax.ppermute(array, 'grid', grid_pairs(lambda zl, x, c: zl * 8 + (x + d)...  16.7 us
    ppermute x12, starting transfers between devices, from_x(): lax.ppermute(array, 'grid', grid_pairs(lambda zl, x, c: zl * 8 + (x + d)...  16.2 us
    dot_general x4, matrix products, apply(): lax.dot_general(rounded, rows, (((0,), (0,)), ((), ())), preferred_elemen...  10.4 us
  transfers between devices with their start and end apart: 34, of which 17 were waited for; matrix products, arithmetic and copies ran while one was open for 12% of the time, Pallas kernels for 0%

commit v1 on v0

--- a/solution.py
+++ b/solution.py
@@ -64,9 +64,9 @@
 def reduce_over_zl(parts):
     zl = position()[0]
     parts = parts.reshape(parts.shape[0], 2, 2, 8, parts.shape[3])
-    for d, bit in ((2, zl // 2), (1, zl % 2)):
-        there = from_zl(pick(parts, 1 - bit, 1).astype(jnp.bfloat16), d)
-        parts = pick(parts, bit, 1) + there.astype(jnp.float32)
+    for d, bit, axis in ((1, zl % 2, 2), (2, zl // 2, 1)):
+        there = from_zl(pick(parts, 1 - bit, axis).astype(jnp.bfloat16), d)
+        parts = pick(parts, bit, axis) + there.astype(jnp.float32)
     return parts
 
 
@@ -82,10 +82,10 @@
 
 def gather_over_grid(rows):
     zl, x, _ = position()
-    there = from_zl(rows, 1)
-    held = placed([(zl % 2, rows), (1 - zl % 2, there)], 1)
-    there = from_zl(held, 2)
-    held = placed([(zl // 2, held), (1 - zl // 2, there)], 1)
+    there = from_zl(rows, 2)
+    held = placed([(zl // 2, rows), (1 - zl // 2, there)], 1)
+    there = from_zl(held, 1)
+    held = placed([(zl % 2, held), (1 - zl % 2, there)], 2)
     held = held.reshape(held.shape[0], ZL, *held.shape[3:])
     there = [((x + d) % NX, from_x(held, d)) for d in (1, 3, 2)]
     held = placed([(x, held)] + there, 1)

time: 210 us -> 206 us (0.981)
  waiting for transfers between devices: 79 us -> 70.8 us
  starting transfers between devices: 97.5 us -> 102 us
    ppermute x6, waiting for transfers between devices: 17.1 us -> 9.48 us  [from_zl(): lax.ppermute(array, 'grid', grid_pairs(lambda zl, x, c: (zl ^ d) * 8 + x...]
    ppermute x6, starting transfers between devices: 20.6 us -> 23.9 us  [from_zl(): lax.ppermute(array, 'grid', grid_pairs(lambda zl, x, c: (zl ^ d) * 8 + x...]
where the time goes in v1:
time: 206 us
  starting transfers between devices  102 us (50%)
  waiting for transfers between devices  70.8 us (34%)
  matrix products  19.3 us (9%)
  local copies, waits for them, and re-layouts  10 us (5%)
  other arithmetic  2.11 us (1%)
    ppermute x12, waiting for transfers between devices, fetch_band(): return lax.ppermute(array, 'band', pairs)  43.1 us
    ppermute x4, starting transfers between devices, from_core(): lax.ppermute(array, 'grid', grid_pairs(lambda zl, x, c: zl * 8 + x * 2 +...  35.5 us
    ppermute x12, starting transfers between devices, fetch_band(): return lax.ppermute(array, 'band', pairs)  26.7 us
    ppermute x6, starting transfers between devices, from_zl(): lax.ppermute(array, 'grid', grid_pairs(lambda zl, x, c: (zl ^ d) * 8 + x...  23.9 us
    ppermute x12, waiting for transfers between devices, from_x(): lax.ppermute(array, 'grid', grid_pairs(lambda zl, x, c: zl * 8 + (x + d)...  16.4 us
    ppermute x12, starting transfers between devices, from_x(): lax.ppermute(array, 'grid', grid_pairs(lambda zl, x, c: zl * 8 + (x + d)...  16.3 us
    dot_general x4, matrix products, apply(): lax.dot_general(rounded, rows, (((0,), (0,)), ((), ())), preferred_elemen...  10.4 us
    ppermute x6, waiting for transfers between devices, from_zl(): lax.ppermute(array, 'grid', grid_pairs(lambda zl, x, c: (zl ^ d) * 8 + x...  9.48 us
  transfers between devices with their start and end apart: 34, of which 17 were waited for; matrix products, arithmetic and copies ran while one was open for 12% of the time, Pallas kernels for 0%

profile of v1, /device:TPU:1, one launch (start us, length us, event | category | flops | bytes accessed | tf_op | source)
XLA Modules:
  0.0 206.0 jit_solution(15237562130128361649)
XLA Ops:
  0.6 7.8 %collective-permute-start.7 = (bf16[256,2048]{1,0:T(8,128)(2,1)}, bf16[256,2048]{1,0:T(8,128)(2,1)S(1)}, u32[]{:S(2)}, u32[]{:S(2)}) collective-permute-start(bf16[256,2048]{1,0:T(8,128)(2,1)} %param.3), channel_id=1, source_target_pairs={{128,0},{160,32},{192,64},{224,96},{0,128},{32,160},{64,192},{96,2... | collective-permute-start | bytes 3145736 | tf_op jit(solution)/shard_map/ppermute | solution.py:17
  8.5 2.7 %collective-permute-start = (bf16[256,2048]{1,0:T(8,128)(2,1)}, bf16[256,2048]{1,0:T(8,128)(2,1)}, u32[]{:S(2)}, u32[]{:S(2)}) collective-permute-start(bf16[256,2048]{1,0:T(8,128)(2,1)} %param.3), channel_id=1, source_target_pairs={{32,0},{64,32},{96,64},{0,96},{160,128},{192,160},{224,192},{128,2... | collective-permute-start | bytes 3145736 | tf_op jit(solution)/shard_map/ppermute | solution.py:17
  14.2 22.8 %collective-permute-done.7 = bf16[256,2048]{1,0:T(8,128)(2,1)S(1)} collective-permute-done((bf16[256,2048]{1,0:T(8,128)(2,1)}, bf16[256,2048]{1,0:T(8,128)(2,1)S(1)}, u32[]{:S(2)}, u32[]{:S(2)}) %collective-permute-start.7) | collective-permute-done | bytes 1048608 | tf_op jit(solution)/shard_map/ppermute | solution.py:17
  47.8 4.7 %collective-permute-done.9 = bf16[256,2048]{1,0:T(8,128)(2,1)S(1)} collective-permute-done((bf16[256,2048]{1,0:T(8,128)(2,1)S(1)}, bf16[256,2048]{1,0:T(8,128)(2,1)S(1)}, u32[]{:S(2)}, u32[]{:S(2)}) %collective-permute-start.9) | collective-permute-done | bytes 1048608 | tf_op jit(solution)/shard_map/ppermute | solution.py:17
  52.6 2.7 %collective-permute-start.10 = (bf16[128,2048]{1,0:T(8,128)(2,1)S(1)}, bf16[128,2048]{1,0:T(8,128)(2,1)S(1)}, u32[]{:S(2)}, u32[]{:S(2)}) collective-permute-start(bf16[128,2048]{1,0:T(8,128)(2,1)S(1)} %slice.288), channel_id=1, source_target_pairs={{32,0},{64,32},{96,64},{0,96},{160,128},{192,160},{224,192},{128,2... | collective-permute-start | bytes 1572872 | tf_op jit(solution)/shard_map/ppermute | solution.py:17
  55.3 13.8 %collective-permute-done.2 = bf16[256,2048]{1,0:T(8,128)(2,1)S(1)} collective-permute-done((bf16[256,2048]{1,0:T(8,128)(2,1)}, bf16[256,2048]{1,0:T(8,128)(2,1)S(1)}, u32[]{:S(2)}, u32[]{:S(2)}) %collective-permute-start.2) | collective-permute-done | bytes 1048608 | tf_op jit(solution)/shard_map/ppermute | solution.py:17
  70.2 23.6 %collective-permute-start.3 = (bf16[4,128,512]{2,1,0:T(8,128)(2,1)S(1)}, bf16[4,128,512]{2,1,0:T(8,128)(2,1)S(1)}, u32[]{:S(2)}, u32[]{:S(2)}) collective-permute-start(bf16[4,128,512]{2,1,0:T(8,128)(2,1)S(1)} %fusion.9), channel_id=1, source_target_pairs={{1,0},{0,1},{3,2},{2,3},{5,4},{4,5},{7,6},{6,7},{9,8},{8,9},{11,10... | collective-permute-start | bytes 1572872 | tf_op jit(solution)/shard_map/ppermute | solution.py:30
  99.4 2.8 %collective-permute-start.6 = (bf16[4,4,8,512]{3,2,1,0:T(8,128)(2,1)S(1)}, bf16[4,4,8,512]{3,2,1,0:T(8,128)(2,1)S(1)}, u32[]{:S(2)}, u32[]{:S(2)}) collective-permute-start(bf16[4,4,8,512]{3,2,1,0:T(8,128)(2,1)S(1)} %get-tuple-element.11), channel_id=1, source_target_pairs={{4,0},{5,1},{6,2},{7,3},{0,4},{1,5},{2,6},{3,7},{12,8},{13,9},{14,... | collective-permute-start | bytes 393224 | tf_op jit(solution)/shard_map/ppermute | solution.py:34
  102.6 2.4 %collective-permute-start.4 = (bf16[4,4,8,512]{3,2,1,0:T(8,128)(2,1)S(1)}, bf16[4,4,8,512]{3,2,1,0:T(8,128)(2,1)S(1)}, u32[]{:S(2)}, u32[]{:S(2)}) collective-permute-start(bf16[4,4,8,512]{3,2,1,0:T(8,128)(2,1)S(1)} %get-tuple-element.10), channel_id=1, source_target_pairs={{2,0},{3,1},{4,2},{5,3},{6,4},{7,5},{0,6},{1,7},{10,8},{11,9},{12,... | collective-permute-start | bytes 393224 | tf_op jit(solution)/shard_map/ppermute | solution.py:34
  106.1 2.5 %collective-permute-start.13 = (bf16[4,4,8,512]{3,2,1,0:T(8,128)(2,1)S(1)}, bf16[4,4,8,512]{3,2,1,0:T(8,128)(2,1)S(1)}, u32[]{:S(2)}, u32[]{:S(2)}) collective-permute-start(bf16[4,4,8,512]{3,2,1,0:T(8,128)(2,1)S(1)} %get-tuple-element.13), channel_id=1, source_target_pairs={{2,0},{3,1},{4,2},{5,3},{6,4},{7,5},{0,6},{1,7},{10,8},{11,9},{12,... | collective-permute-start | bytes 393224 | tf_op jit(solution)/shard_map/ppermute | solution.py:34
  111.2 3.5 %collective-permute-done.14 = bf16[4,4,8,512]{3,2,1,0:T(8,128)(2,1)S(1)} collective-permute-done((bf16[4,4,8,512]{3,2,1,0:T(8,128)(2,1)S(1)}, bf16[4,4,8,512]{3,2,1,0:T(8,128)(2,1)S(1)}, u32[]{:S(2)}, u32[]{:S(2)}) %collective-permute-start.14) | collective-permute-done | bytes 131104 | tf_op jit(solution)/shard_map/ppermute | solution.py:34
  114.9 17.4 %collective-permute-start.16 = (bf16[8,2,8,512]{3,2,0,1:T(8,128)(2,1)S(1)}, bf16[8,2,8,512]{3,2,0,1:T(8,128)(2,1)S(1)}, u32[]{:S(2)}, u32[]{:S(2)}) collective-permute-start(bf16[8,2,8,512]{3,2,0,1:T(8,128)(2,1)S(1)} %fusion.16), channel_id=1, source_target_pairs={{8,0},{9,1},{10,2},{11,3},{12,4},{13,5},{14,6},{15,7},{0,8},{1,9},... | collective-permute-start | bytes 393224 | tf_op jit(solution)/shard_map/ppermute | solution.py:40
  132.4 3.1 %collective-permute-done.16 = bf16[8,2,8,512]{3,2,0,1:T(8,128)(2,1)S(1)} collective-permute-done((bf16[8,2,8,512]{3,2,0,1:T(8,128)(2,1)S(1)}, bf16[8,2,8,512]{3,2,0,1:T(8,128)(2,1)S(1)}, u32[]{:S(2)}, u32[]{:S(2)}) %collective-permute-start.16) | collective-permute-done | bytes 131104 | tf_op jit(solution)/shard_map/ppermute | solution.py:40
  137.5 4.1 %constant_dynamic-slice_fusion.1 = (bf16[8,1,128,2048]{3,2,1,0:T(8,128)(2,1)}, bf16[8,1,128,2048]{3,2,1,0:T(8,128)(2,1)}) fusion(bf16[8,2,128,2048]{3,2,1,0:T(8,128)(2,1)S(1)} %bitcast.216, s32[]{:T(128)S(6)} %select_n.218, s32[]{:T(128)S(6)} %select_n.219), kind=kLoop, calls=%fused_computation.148 | loop fusion | bytes 16777224 | tf_op jit(solution)/shard_map/jit(dynamic_index_in_dim)/dynamic_slice | solution.py:49
  142.3 5.0 %collective-permute-start.24 = (bf16[2,4,8,256]{3,2,1,0:T(8,128)(2,1)S(1)}, bf16[2,4,8,256]{3,2,1,0:T(8,128)(2,1)S(1)}, u32[]{:S(2)}, u32[]{:S(2)}) collective-permute-start(bf16[2,4,8,256]{3,2,1,0:T(8,128)(2,1)S(1)} %bitcast.248), channel_id=1, source_target_pairs={{128,0},{160,32},{192,64},{224,96},{0,128},{32,160},{64,192},{96,2... | collective-permute-start | bytes 98312 | tf_op jit(solution)/shard_map/ppermute | solution.py:17
  149.2 2.7 %collective-permute-start.25 = (bf16[2,2,4,8,256]{4,3,2,1,0:T(8,128)(2,1)S(1)}, bf16[2,2,4,8,256]{4,3,2,1,0:T(8,128)(2,1)S(1)}, u32[]{:S(2)}, u32[]{:S(2)}) collective-permute-start(bf16[2,2,4,8,256]{4,3,2,1,0:T(8,128)(2,1)S(1)} %pad_maximum_fusion.4), channel_id=1, source_target_pairs={{32,0},{64,32},{96,64},{0,96},{160,128},{192,160},{224,192},{128,2... | collective-permute-start | bytes 196616 | tf_op jit(solution)/shard_map/ppermute | solution.py:17
  156.3 3.2 %collective-permute-start.20 = (bf16[8,4,8,256]{3,2,1,0:T(8,128)(2,1)S(1)}, bf16[8,4,8,256]{3,2,1,0:T(8,128)(2,1)S(1)}, u32[]{:S(2)}, u32[]{:S(2)}) collective-permute-start(bf16[8,4,8,256]{3,2,1,0:T(8,128)(2,1)S(1)} %bitcast.241), channel_id=1, source_target_pairs={{2,0},{3,1},{4,2},{5,3},{6,4},{7,5},{0,6},{1,7},{10,8},{11,9},{12,... | collective-permute-start | bytes 393224 | tf_op jit(solution)/shard_map/ppermute | solution.py:34
  161.4 4.5 %collective-permute-done.21 = bf16[8,4,8,256]{3,2,1,0:T(8,128)(2,1)S(1)} collective-permute-done((bf16[8,4,8,256]{3,2,1,0:T(8,128)(2,1)S(1)}, bf16[8,4,8,256]{3,2,1,0:T(8,128)(2,1)S(1)}, u32[]{:S(2)}, u32[]{:S(2)}) %collective-permute-start.21) | collective-permute-done | bytes 131104 | tf_op jit(solution)/shard_map/ppermute | solution.py:34
  165.9 6.3 %collective-permute-start.23 = (bf16[8,4,4,8,256]{4,3,2,1,0:T(8,128)(2,1)S(1)}, bf16[8,4,4,8,256]{4,3,2,1,0:T(8,128)(2,1)S(1)}, u32[]{:S(2)}, u32[]{:S(2)}) collective-permute-start(bf16[8,4,4,8,256]{4,3,2,1,0:T(8,128)(2,1)S(1)} %bitcast_dynamic-update-slice_fusion.4), channel_id=1, source_target_pairs={{1,0},{0,1},{3,2},{2,3},{5,4},{4,5},{7,6},{6,7},{9,8},{8,9},{11,10... | collective-permute-start | bytes 1572872 | tf_op jit(solution)/shard_map/ppermute | solution.py:30
  173.8 2.6 %fusion.41 = f32[256,2048]{1,0:T(8,128)} fusion(bf16[1024,256]{1,0:T(8,128)(2,1)S(1)} %bitcast.238, bf16[1024,2048]{1,0:T(8,128)(2,1)S(1)} %bitcast.223), kind=kOutput, calls=%fused_computation.165 | convolution fusion | flops 1073741824 | bytes 6815744 | tf_op jit(solution)/shard_map/dot_general | solution.py:102
  181.6 2.3 %collective-permute-done.29 = bf16[9,2,8,256]{3,2,1,0:T(8,128)(2,1)S(1)} collective-permute-done((bf16[9,2,8,256]{3,2,1,0:T(8,128)(2,1)S(1)}, bf16[9,2,8,256]{3,2,1,0:T(8,128)(2,1)S(1)}, u32[]{:S(2)}, u32[]{:S(2)}) %collective-permute-start.29) | collective-permute-done | bytes 73760 | tf_op jit(solution)/shard_map/ppermute | solution.py:40
  185.8 4.3 %fusion.1 = f32[256,2048]{1,0:T(8,128)S(1)} fusion(f32[256,2048]{1,0:T(8,128)} %fusion.41, bf16[1024,256]{1,0:T(8,128)(2,1)S(1)} %bitcast.218, bf16[1024,2048]{1,0:T(8,128)(2,1)} %bitcast.214, bf16[256,2048]{1,0:T(8,128)(2,1)S(1)} %copy-done.1), kind=kOutput, calls=%fused_computation.5 | convolution fusion | flops 1075838976 | bytes 9961472 | tf_op jit(solution)/shard_map/dot_general | solution.py:102
  191.6 5.5 %collective-permute-done.31 = bf16[9,4,8,256]{3,2,1,0:T(8,128)(2,1)S(1)} collective-permute-done((bf16[9,4,8,256]{3,2,1,0:T(8,128)(2,1)S(1)}, bf16[9,4,8,256]{3,2,1,0:T(8,128)(2,1)S(1)}, u32[]{:S(2)}, u32[]{:S(2)}) %collective-permute-start.31) | collective-permute-done | bytes 147488 | tf_op jit(solution)/shard_map/ppermute | solution.py:34
  197.1 4.3 %collective-permute-start.33 = (bf16[9,4,4,8,256]{4,3,2,1,0:T(8,128)(2,1)S(1)}, bf16[9,4,4,8,256]{4,3,2,1,0:T(8,128)(2,1)S(1)}, u32[]{:S(2)}, u32[]{:S(2)}) collective-permute-start(bf16[9,4,4,8,256]{4,3,2,1,0:T(8,128)(2,1)S(1)} %bitcast_dynamic-update-slice_fusion), channel_id=1, source_target_pairs={{1,0},{0,1},{3,2},{2,3},{5,4},{4,5},{7,6},{6,7},{9,8},{8,9},{11,10... | collective-permute-start | bytes 1769480 | tf_op jit(solution)/shard_map/ppermute | solution.py:30
  (160 shorter events, 49.9 us)
Async XLA Ops:
  0.6 36.4 %collective-permute-start.7 = (bf16[256,2048]{1,0:T(8,128)(2,1)}, bf16[256,2048]{1,0:T(8,128)(2,1)S(1)}, u32[]{:S(2)}, u32[]{:S(2)}) collective-permute-start(bf16[256,2048]{1,0:T(8,128)(2,1)} %param.3), channel_id=1, source_target_pairs={{128,0},{160,32},{192,64},{224,96},{0,128},{32,160},{64,192},{96,2... | collective-permute-start | bytes 3145736 | tf_op jit(solution)/shard_map/ppermute | solution.py:17
  8.5 31.8 %collective-permute-start = (bf16[256,2048]{1,0:T(8,128)(2,1)}, bf16[256,2048]{1,0:T(8,128)(2,1)}, u32[]{:S(2)}, u32[]{:S(2)}) collective-permute-start(bf16[256,2048]{1,0:T(8,128)(2,1)} %param.3), channel_id=1, source_target_pairs={{32,0},{64,32},{96,64},{0,96},{160,128},{192,160},{224,192},{128,2... | collective-permute-start | bytes 3145736 | tf_op jit(solution)/shard_map/ppermute | solution.py:17
  11.2 34.6 %collective-permute-start.1 = (bf16[256,2048]{1,0:T(8,128)(2,1)}, bf16[256,2048]{1,0:T(8,128)(2,1)}, u32[]{:S(2)}, u32[]{:S(2)}) collective-permute-start(bf16[256,2048]{1,0:T(8,128)(2,1)} %param.3), channel_id=1, source_target_pairs={{96,0},{0,32},{32,64},{64,96},{224,128},{128,160},{160,192},{192,2... | collective-permute-start | bytes 3145736 | tf_op jit(solution)/shard_map/ppermute | solution.py:17
  37.1 15.4 %collective-permute-start.9 = (bf16[256,2048]{1,0:T(8,128)(2,1)S(1)}, bf16[256,2048]{1,0:T(8,128)(2,1)S(1)}, u32[]{:S(2)}, u32[]{:S(2)}) collective-permute-start(bf16[256,2048]{1,0:T(8,128)(2,1)S(1)} %collective-permute-done.7), channel_id=1, source_target_pairs={{96,0},{0,32},{32,64},{64,96},{224,128},{128,160},{160,192},{192,2... | collective-permute-start | bytes 3145736 | tf_op jit(solution)/shard_map/ppermute | solution.py:17
  38.8 13.8 %collective-permute-start.8 = (bf16[256,2048]{1,0:T(8,128)(2,1)S(1)}, bf16[256,2048]{1,0:T(8,128)(2,1)S(1)}, u32[]{:S(2)}, u32[]{:S(2)}) collective-permute-start(bf16[256,2048]{1,0:T(8,128)(2,1)S(1)} %collective-permute-done.7), channel_id=1, source_target_pairs={{32,0},{64,32},{96,64},{0,96},{160,128},{192,160},{224,192},{128,2... | collective-permute-start | bytes 3145736 | tf_op jit(solution)/shard_map/ppermute | solution.py:17
  40.3 28.9 %collective-permute-start.2 = (bf16[256,2048]{1,0:T(8,128)(2,1)}, bf16[256,2048]{1,0:T(8,128)(2,1)S(1)}, u32[]{:S(2)}, u32[]{:S(2)}) collective-permute-start(bf16[256,2048]{1,0:T(8,128)(2,1)} %collective-permute-done), channel_id=1, source_target_pairs={{32,0},{64,32},{96,64},{0,96},{160,128},{192,160},{224,192},{128,2... | collective-permute-start | bytes 3145736 | tf_op jit(solution)/shard_map/ppermute | solution.py:17
  52.5 44.4 %collective-permute-start.11 = (bf16[128,2048]{1,0:T(8,128)(2,1)S(1)}, bf16[128,2048]{1,0:T(8,128)(2,1)S(1)}, u32[]{:S(2)}, u32[]{:S(2)}) collective-permute-start(bf16[128,2048]{1,0:T(8,128)(2,1)S(1)} %slice.289), channel_id=1, source_target_pairs={{96,0},{0,32},{32,64},{64,96},{224,128},{128,160},{160,192},{192,2... | collective-permute-start | bytes 1572872 | tf_op jit(solution)/shard_map/ppermute | solution.py:17
  52.6 44.3 %collective-permute-start.10 = (bf16[128,2048]{1,0:T(8,128)(2,1)S(1)}, bf16[128,2048]{1,0:T(8,128)(2,1)S(1)}, u32[]{:S(2)}, u32[]{:S(2)}) collective-permute-start(bf16[128,2048]{1,0:T(8,128)(2,1)S(1)} %slice.288), channel_id=1, source_target_pairs={{32,0},{64,32},{96,64},{0,96},{160,128},{192,160},{224,192},{128,2... | collective-permute-start | bytes 1572872 | tf_op jit(solution)/shard_map/ppermute | solution.py:17
  70.2 29.0 %collective-permute-start.3 = (bf16[4,128,512]{2,1,0:T(8,128)(2,1)S(1)}, bf16[4,128,512]{2,1,0:T(8,128)(2,1)S(1)}, u32[]{:S(2)}, u32[]{:S(2)}) collective-permute-start(bf16[4,128,512]{2,1,0:T(8,128)(2,1)S(1)} %fusion.9), channel_id=1, source_target_pairs={{1,0},{0,1},{3,2},{2,3},{5,4},{4,5},{7,6},{6,7},{9,8},{8,9},{11,10... | collective-permute-start | bytes 1572872 | tf_op jit(solution)/shard_map/ppermute | solution.py:30
  97.9 7.1 %collective-permute-start.12 = (bf16[4,128,512]{2,1,0:T(8,128)(2,1)S(1)}, bf16[4,128,512]{2,1,0:T(8,128)(2,1)S(1)}, u32[]{:S(2)}, u32[]{:S(2)}) collective-permute-start(bf16[4,128,512]{2,1,0:T(8,128)(2,1)S(1)} %fusion.10), channel_id=1, source_target_pairs={{1,0},{0,1},{3,2},{2,3},{5,4},{4,5},{7,6},{6,7},{9,8},{8,9},{11,10... | collective-permute-start | bytes 1572872 | tf_op jit(solution)/shard_map/ppermute | solution.py:30
  99.4 6.6 %collective-permute-start.6 = (bf16[4,4,8,512]{3,2,1,0:T(8,128)(2,1)S(1)}, bf16[4,4,8,512]{3,2,1,0:T(8,128)(2,1)S(1)}, u32[]{:S(2)}, u32[]{:S(2)}) collective-permute-start(bf16[4,4,8,512]{3,2,1,0:T(8,128)(2,1)S(1)} %get-tuple-element.11), channel_id=1, source_target_pairs={{4,0},{5,1},{6,2},{7,3},{0,4},{1,5},{2,6},{3,7},{12,8},{13,9},{14,... | collective-permute-start | bytes 393224 | tf_op jit(solution)/shard_map/ppermute | solution.py:34
  102.3 6.8 %collective-permute-start.5 = (bf16[4,4,8,512]{3,2,1,0:T(8,128)(2,1)S(1)}, bf16[4,4,8,512]{3,2,1,0:T(8,128)(2,1)S(1)}, u32[]{:S(2)}, u32[]{:S(2)}) collective-permute-start(bf16[4,4,8,512]{3,2,1,0:T(8,128)(2,1)S(1)} %get-tuple-element.12), channel_id=1, source_target_pairs={{6,0},{7,1},{0,2},{1,3},{2,4},{3,5},{4,6},{5,7},{14,8},{15,9},{8,1... | collective-permute-start | bytes 393224 | tf_op jit(solution)/shard_map/ppermute | solution.py:34
  105.4 9.3 %collective-permute-start.14 = (bf16[4,4,8,512]{3,2,1,0:T(8,128)(2,1)S(1)}, bf16[4,4,8,512]{3,2,1,0:T(8,128)(2,1)S(1)}, u32[]{:S(2)}, u32[]{:S(2)}) collective-permute-start(bf16[4,4,8,512]{3,2,1,0:T(8,128)(2,1)S(1)} %get-tuple-element.14), channel_id=1, source_target_pairs={{6,0},{7,1},{0,2},{1,3},{2,4},{3,5},{4,6},{5,7},{14,8},{15,9},{8,1... | collective-permute-start | bytes 393224 | tf_op jit(solution)/shard_map/ppermute | solution.py:34
  106.1 8.7 %collective-permute-start.13 = (bf16[4,4,8,512]{3,2,1,0:T(8,128)(2,1)S(1)}, bf16[4,4,8,512]{3,2,1,0:T(8,128)(2,1)S(1)}, u32[]{:S(2)}, u32[]{:S(2)}) collective-permute-start(bf16[4,4,8,512]{3,2,1,0:T(8,128)(2,1)S(1)} %get-tuple-element.13), channel_id=1, source_target_pairs={{2,0},{3,1},{4,2},{5,3},{6,4},{7,5},{0,6},{1,7},{10,8},{11,9},{12,... | collective-permute-start | bytes 393224 | tf_op jit(solution)/shard_map/ppermute | solution.py:34
  114.9 20.5 %collective-permute-start.16 = (bf16[8,2,8,512]{3,2,0,1:T(8,128)(2,1)S(1)}, bf16[8,2,8,512]{3,2,0,1:T(8,128)(2,1)S(1)}, u32[]{:S(2)}, u32[]{:S(2)}) collective-permute-start(bf16[8,2,8,512]{3,2,0,1:T(8,128)(2,1)S(1)} %fusion.16), channel_id=1, source_target_pairs={{8,0},{9,1},{10,2},{11,3},{12,4},{13,5},{14,6},{15,7},{0,8},{1,9},... | collective-permute-start | bytes 393224 | tf_op jit(solution)/shard_map/ppermute | solution.py:40
  141.8 11.0 %collective-permute-start.18 = (bf16[8,8,256]{2,1,0:T(8,128)(2,1)S(1)}, bf16[8,8,256]{2,1,0:T(8,128)(2,1)S(1)}, u32[]{:S(2)}, u32[]{:S(2)}) collective-permute-start(bf16[8,8,256]{2,1,0:T(8,128)(2,1)S(1)} %get-tuple-element.5), channel_id=1, source_target_pairs={{16,0},{17,1},{18,2},{19,3},{20,4},{21,5},{22,6},{23,7},{24,8},{25... | collective-permute-start | bytes 98312 | tf_op jit(solution)/shard_map/ppermute | solution.py:40
  142.3 6.9 %collective-permute-start.24 = (bf16[2,4,8,256]{3,2,1,0:T(8,128)(2,1)S(1)}, bf16[2,4,8,256]{3,2,1,0:T(8,128)(2,1)S(1)}, u32[]{:S(2)}, u32[]{:S(2)}) collective-permute-start(bf16[2,4,8,256]{3,2,1,0:T(8,128)(2,1)S(1)} %bitcast.248), channel_id=1, source_target_pairs={{128,0},{160,32},{192,64},{224,96},{0,128},{32,160},{64,192},{96,2... | collective-permute-start | bytes 98312 | tf_op jit(solution)/shard_map/ppermute | solution.py:17
  149.2 10.3 %collective-permute-start.25 = (bf16[2,2,4,8,256]{4,3,2,1,0:T(8,128)(2,1)S(1)}, bf16[2,2,4,8,256]{4,3,2,1,0:T(8,128)(2,1)S(1)}, u32[]{:S(2)}, u32[]{:S(2)}) collective-permute-start(bf16[2,2,4,8,256]{4,3,2,1,0:T(8,128)(2,1)S(1)} %pad_maximum_fusion.4), channel_id=1, source_target_pairs={{32,0},{64,32},{96,64},{0,96},{160,128},{192,160},{224,192},{128,2... | collective-permute-start | bytes 196616 | tf_op jit(solution)/shard_map/ppermute | solution.py:17
  151.9 8.9 %collective-permute-start.26 = (bf16[2,2,4,8,256]{4,3,2,1,0:T(8,128)(2,1)S(1)}, bf16[2,2,4,8,256]{4,3,2,1,0:T(8,128)(2,1)S(1)}, u32[]{:S(2)}, u32[]{:S(2)}) collective-permute-start(bf16[2,2,4,8,256]{4,3,2,1,0:T(8,128)(2,1)S(1)} %pad_maximum_fusion.4), channel_id=1, source_target_pairs={{64,0},{96,32},{0,64},{32,96},{192,128},{224,160},{128,192},{160,2... | collective-permute-start | bytes 196616 | tf_op jit(solution)/shard_map/ppermute | solution.py:17
  152.3 8.4 %collective-permute-start.27 = (bf16[2,2,4,8,256]{4,3,2,1,0:T(8,128)(2,1)S(1)}, bf16[2,2,4,8,256]{4,3,2,1,0:T(8,128)(2,1)S(1)}, u32[]{:S(2)}, u32[]{:S(2)}) collective-permute-start(bf16[2,2,4,8,256]{4,3,2,1,0:T(8,128)(2,1)S(1)} %pad_maximum_fusion.4), channel_id=1, source_target_pairs={{96,0},{0,32},{32,64},{64,96},{224,128},{128,160},{160,192},{192,2... | collective-permute-start | bytes 196616 | tf_op jit(solution)/shard_map/ppermute | solution.py:17
  165.9 7.9 %collective-permute-start.23 = (bf16[8,4,4,8,256]{4,3,2,1,0:T(8,128)(2,1)S(1)}, bf16[8,4,4,8,256]{4,3,2,1,0:T(8,128)(2,1)S(1)}, u32[]{:S(2)}, u32[]{:S(2)}) collective-permute-start(bf16[8,4,4,8,256]{4,3,2,1,0:T(8,128)(2,1)S(1)} %bitcast_dynamic-update-slice_fusion.4), channel_id=1, source_target_pairs={{1,0},{0,1},{3,2},{2,3},{5,4},{4,5},{7,6},{6,7},{9,8},{8,9},{11,10... | collective-permute-start | bytes 1572872 | tf_op jit(solution)/shard_map/ppermute | solution.py:30
  184.0 7.6 %collective-permute-start.30 = (bf16[9,4,8,256]{3,2,1,0:T(8,128)(2,1)S(1)}, bf16[9,4,8,256]{3,2,1,0:T(8,128)(2,1)S(1)}, u32[]{:S(2)}, u32[]{:S(2)}) collective-permute-start(bf16[9,4,8,256]{3,2,1,0:T(8,128)(2,1)S(1)} %bitcast.232), channel_id=1, source_target_pairs={{2,0},{3,1},{4,2},{5,3},{6,4},{7,5},{0,6},{1,7},{10,8},{11,9},{12,... | collective-permute-start | bytes 442376 | tf_op jit(solution)/shard_map/ppermute | solution.py:34
  190.1 6.9 %collective-permute-start.31 = (bf16[9,4,8,256]{3,2,1,0:T(8,128)(2,1)S(1)}, bf16[9,4,8,256]{3,2,1,0:T(8,128)(2,1)S(1)}, u32[]{:S(2)}, u32[]{:S(2)}) collective-permute-start(bf16[9,4,8,256]{3,2,1,0:T(8,128)(2,1)S(1)} %bitcast.233), channel_id=1, source_target_pairs={{6,0},{7,1},{0,2},{1,3},{2,4},{3,5},{4,6},{5,7},{14,8},{15,9},{8,1... | collective-permute-start | bytes 442376 | tf_op jit(solution)/shard_map/ppermute | solution.py:34
  190.2 6.8 %collective-permute-start.32 = (bf16[9,4,8,256]{3,2,1,0:T(8,128)(2,1)S(1)}, bf16[9,4,8,256]{3,2,1,0:T(8,128)(2,1)S(1)}, u32[]{:S(2)}, u32[]{:S(2)}) collective-permute-start(bf16[9,4,8,256]{3,2,1,0:T(8,128)(2,1)S(1)} %bitcast.234), channel_id=1, source_target_pairs={{4,0},{5,1},{6,2},{7,3},{0,4},{1,5},{2,6},{3,7},{12,8},{13,9},{14,... | collective-permute-start | bytes 442376 | tf_op jit(solution)/shard_map/ppermute | solution.py:34
  (15 other events, 116.0 us)
